TPU v7x, 256 devices: a whole 4x4x8 slice. The times are simulated.
256 devices in a mesh: row: 32 (over y, x, core), col: 8 (over z).
Axes of the slice: x: 4, y: 4, z: 8, core: 2. Of those that a mesh axis runs over, the one named last changes fastest.
Arguments:
- integrals: bfloat16 [1280, 32, 8192], P('row', None, 'col'), may hold values from -6 to 6
- coeffs: bfloat16 [40960, 4096], P('row', 'col'), may hold values from -0.0546875 to 0.0546875
- mask: int32 [1280, 8], replicated, may hold values from 0 to 1, as said below
- offsets: int32 [1281], replicated, may hold values from 0 to 30720, as said below
- atom_of_slot: int32 [1280], replicated, may hold values from 0 to 1279, as said below
Outputs:
- half_transformed: bfloat16 [4096, 8192], P('row', 'col')
Inputs may be any that keep to these rules, and one draw needn't show every extreme that they name: `mask`: 1 marks a significant pair of an atom and a block of 64 window functions. offsets[0] = 0 and offsets[a + 1] - offsets[a] is atom a's number of basis functions, 16 to 32; atoms 2k and 2k + 1 together have 3 * 16; rows of an atom's padded block past its number are padding. `atom_of_slot`: a permutation of the atoms; slot k is held by atom owner k // 40 along row, and atom a's AO-row owner is a // 40; one atom owner holds at least one and at most 2 atoms of any one AO-row owner, and exactly 2 for some pairs.
All inputs are finite; a program needn't handle non-finite values.
Results may differ from a plain program's by a relative error of at most 0.015.
Values may be sent and summed in bfloat16 or wider, within the bound.
A program may use at most 256 MiB of HBM per device.

v0:
```python
import jax
import jax.numpy as jnp
from jax import lax
from jax.sharding import PartitionSpec as P


def body(integrals, coeffs, mask, offsets, atom_of_slot):
    n_row = lax.axis_size("row")
    own_row = lax.axis_index("row")
    own_col = lax.axis_index("col")
    per_dev, atom_w, row_width = integrals.shape
    slots_cap = max(2, -(-per_dev // n_row))
    counter = jnp.arange(per_dev, dtype=jnp.int32)
    slot_count = n_row * slots_cap
    mine_slots = lax.dynamic_slice_in_dim(atom_of_slot, own_row * per_dev, per_dev)
    target = mine_slots // per_dev
    before = (target[None, :] == target[:, None]) & (counter[None, :] < counter[:, None])
    arrival_rank = jnp.sum(before.astype(jnp.int32), axis=1)
    position = target * slots_cap + arrival_rank
    placing = (jnp.arange(slot_count, dtype=jnp.int32)[:, None] == position[None, :]).astype(
        jnp.bfloat16
    )
    outgoing = jnp.dot(
        placing, integrals.reshape(per_dev, atom_w * row_width), preferred_element_type=jnp.bfloat16
    )
    outgoing = outgoing.reshape(n_row, slots_cap, atom_w * row_width)
    incoming = lax.all_to_all(outgoing, "row", split_axis=0, concat_axis=0, tiled=True)
    holders = atom_of_slot.reshape(n_row, per_dev)
    is_mine = holders // per_dev == own_row
    arrival = jnp.cumsum(is_mine.astype(jnp.int32), axis=1) - 1
    slot_of = jnp.arange(n_row, dtype=jnp.int32)[:, None] * slots_cap + arrival
    local_atom = holders - own_row * per_dev
    pick_atom = (
        (local_atom.reshape(-1)[:, None] == counter[None, :]) & is_mine.reshape(-1)[:, None]
    ).astype(jnp.float32)
    pick_slot = (
        slot_of.reshape(-1)[:, None] == jnp.arange(slot_count, dtype=jnp.int32)[None, :]
    ).astype(jnp.float32)
    gather_matrix = jnp.dot(pick_atom.T, pick_slot).astype(jnp.bfloat16)
    ordered = jnp.dot(
        gather_matrix,
        incoming.reshape(slot_count, atom_w * row_width),
        preferred_element_type=jnp.bfloat16,
    )
    ordered = ordered.reshape(per_dev, atom_w, row_width)
    bounds = lax.dynamic_slice_in_dim(offsets, own_row * per_dev, per_dev + 1)
    lengths = bounds[1:] - bounds[:-1]
    significant = lax.dynamic_slice(mask, (own_row * per_dev, own_col), (per_dev, 1))[:, 0] > 0
    keep_rows = (jnp.arange(atom_w, dtype=jnp.int32)[None, :] < lengths[:, None]) & significant[
        :, None
    ]
    blocks = ordered * keep_rows[:, :, None].astype(jnp.bfloat16)
    bucket_edges = [0, per_dev]
    kept_rows = blocks.reshape(per_dev * atom_w, row_width)
    coeff_piece = lax.all_gather(coeffs, "col", axis=1, tiled=True)
    low_row = bucket_edges[0] * atom_w
    high_row = bucket_edges[1] * atom_w

    def product(low_row=low_row, high_row=high_row):
        return lax.dot_general(
            coeff_piece, kept_rows, (((0,), (0,)), ((), ())), preferred_element_type=jnp.float32
        )

    bucket_term = product()
    partial_sums = bucket_term.astype(jnp.bfloat16)
    result = lax.psum_scatter(partial_sums, "row", scatter_dimension=0, tiled=True).astype(
        jnp.float32
    )
    return result.astype(jnp.bfloat16)


def solution(mesh):
    in_specs = (P("row", None, "col"), P("row", "col"), P(), P(), P())
    out_specs = P("row", "col")
    return jax.shard_map(body, mesh=mesh, in_specs=in_specs, out_specs=out_specs, check_vma=False)
```

profile of v0, /device:TPU:1, one launch (start us, length us, event | category | flops | bytes accessed | tf_op | source)
XLA Modules:
  0.0 259.7 jit_solution(1185108357489608472)
XLA Ops:
  6.5 0.0 copy-start
  6.5 0.0 all-gather.2.cloned.1.call-start
  6.5 0.7 all-gather.2.cloned.1.call-update
  7.3 5.3 %reshape.121 = bf16[40,32768,1]{1,0,2:T(8,128)(2,1)} reshape(bf16[40,32,1024]{2,1,0:T(8,128)(2,1)} %param.5) | data formatting | bytes 5242880 | tf_op jit(solution)/shard_map/reshape | solution.py:24
  12.5 0.0 copy-done
  12.6 0.1 and_select_fusion
  12.6 0.2 convert_reduce_fusion
  12.8 0.1 multiply_add_fusion.1
  12.9 3.0 %fusion.17 = bf16[32,2,32768]{2,0,1:T(8,128)(2,1)S(1)} fusion(bf16[40,32768,1]{1,0,2:T(8,128)(2,1)} %reshape.121, s32[40]{0:T(128)S(1)} %multiply_add_fusion.1, s32[32,2]{0,1:T(2,128)S(1)} %multiply_add_fusion), kind=kOutput, calls=%fused_computation.13 | convolution fusion | flops 167774720 | bytes 6816160 | tf_op jit(solution)/shard_map/dot_general | solution.py:23
  15.9 6.3 %copy.15 = bf16[32,2,32768]{2,1,0:T(2,128)(2,1)} copy(bf16[32,2,32768]{2,0,1:T(8,128)(2,1)S(1)} %fusion.17) | data formatting | bytes 8388608 | tf_op jit(solution)/shard_map/dot_general | solution.py:23
  22.2 8.6 %all-to-all-start = ((bf16[32,2,32768]{2,1,0:T(2,128)(2,1)}), bf16[32,2,32768]{2,1,0:T(2,128)(2,1)}, u32[]{:S(2)}, u32[]{:S(2)}) async-start(bf16[32,2,32768]{2,1,0:T(2,128)(2,1)} %copy.15), calls=%async_computation | async-start | bytes 8388608 | tf_op jit(solution)/shard_map/all_to_all | solution.py:27
  30.9 0.2 reduce-scatter.4.cloned.1.call-start
  31.1 0.1 and.41
  31.2 0.1 div.18
  31.3 0.2 reduce_window_sum.11
  31.5 0.1 add_add_fusion
  31.6 0.1 add.46
  31.7 0.8 dynamic_slice.10
  32.5 0.8 compare_bitcast_fusion
  33.3 0.1 slice_subtract_fusion
  33.3 48.2 %all-to-all-done = bf16[32,2,32768]{2,1,0:T(2,128)(2,1)} async-done(((bf16[32,2,32768]{2,1,0:T(2,128)(2,1)}), bf16[32,2,32768]{2,1,0:T(2,128)(2,1)}, u32[]{:S(2)}, u32[]{:S(2)}) %all-to-all-start) | async-done | bytes 4194336 | tf_op jit(solution)/shard_map/all_to_all | solution.py:27
  81.5 7.2 %reshape.119 = bf16[64,32768]{1,0:T(8,128)(2,1)} reshape(bf16[32,2,32768]{2,1,0:T(2,128)(2,1)} %all-to-all-done) | data formatting | bytes 8388608 | tf_op jit(solution)/shard_map/reshape | solution.py:42
  88.8 3.9 %fusion.3 = bf16[40,32,1024]{2,0,1:T(8,128)(2,1)S(1)} fusion(bf16[8,32,8,1024]{3,2,1,0:T(8,128)(2,1)} %bitcast.20, bf16[40,32]{0,1:T(8,128)(2,1)S(1)} %fusion.24, s32[1280]{0:T(1024)S(1)} %add.46, s32[1280]{0:T(1024)S(1)} %get-tuple-element.7, pred[1280]{0:T(1024)(128)(4,1)S(1)} %get-tuple-element.5), kind=kOutput, calls=%fused_computation.4 | convolution fusion | flops 179755520 | bytes 6829824 | tf_op jit(solution)/shard_map/dot_general | solution.py:40
  92.7 2.9 %copy.17 = bf16[40,32,1024]{2,1,0:T(8,128)(2,1)} copy(bf16[40,32,1024]{2,0,1:T(8,128)(2,1)S(1)} %fusion.3) | data formatting | bytes 5242880 | tf_op jit(solution)/shard_map/mul | solution.py:52
  95.6 30.9 %all-gather.2.cloned.1.call-done = bf16[1280,4096]{1,0:T(8,128)(2,1)} async-done(((bf16[1280,512]{1,0:T(8,128)(2,1)}), bf16[1280,4096]{1,0:T(8,128)(2,1)}) %all-gather.2.cloned.1.call-update) | async-done | bytes 10485776 | tf_op jit(solution)/shard_map/all_gather | solution.py:55
  126.5 16.8 %convert_bitcast_fusion = bf16[4096,1024]{0,1:T(8,128)(2,1)} fusion(bf16[1280,1024]{1,0:T(8,128)(2,1)} %bitcast.21, bf16[1280,4096]{1,0:T(8,128)(2,1)} %all-gather.2.cloned.1.call-done), kind=kOutput, calls=%fused_computation | convolution fusion | flops 10741612544 | bytes 21495808 | tf_op jit(solution)/shard_map/dot_general | solution.py:60
  143.3 12.0 %copy.19 = bf16[4096,1024]{1,0:T(8,128)(2,1)} copy(bf16[4096,1024]{0,1:T(8,128)(2,1)} %convert_bitcast_fusion) | data formatting | bytes 16777216
  155.3 0.0 reduce-scatter.4.cloned.1.call-update
  155.3 97.5 %reduce-scatter.4.cloned.1.call-done = bf16[128,1024]{1,0:T(8,128)(2,1)} async-done(((bf16[4096,1024]{1,0:T(8,128)(2,1)}), bf16[128,1024]{1,0:T(8,128)(2,1)}) %reduce-scatter.4.cloned.1.call-update) | async-done | bytes 262160 | tf_op jit(solution)/shard_map/reduce_scatter | solution.py:66
  (6 shorter events, 0.1 us)
Async XLA Ops:
  6.5 6.0 %copy-start = (s32[1280]{0:T(1024)S(1)}, s32[1280]{0:T(1024)}, u32[]{:S(2)}) copy-start(s32[1280]{0:T(1024)} %param.9) | copy-start | bytes 15364
  6.5 120.0 %all-gather.2.cloned.1.call-start = ((), (), s32[]{:S(2)}) async-start(), calls=%async_computation.2 | async-start | bytes 11796480 | tf_op jit(solution)/shard_map/all_gather | solution.py:55
  22.2 59.3 %all-to-all-start = ((bf16[32,2,32768]{2,1,0:T(2,128)(2,1)}), bf16[32,2,32768]{2,1,0:T(2,128)(2,1)}, u32[]{:S(2)}, u32[]{:S(2)}) async-start(bf16[32,2,32768]{2,1,0:T(2,128)(2,1)} %copy.15), calls=%async_computation | async-start | bytes 8388608 | tf_op jit(solution)/shard_map/all_to_all | solution.py:27
  30.9 221.9 %reduce-scatter.4.cloned.1.call-start = ((), (), s32[]{:S(2)}) async-start(), calls=%async_computation.3 | async-start | bytes 8650752 | tf_op jit(solution)/shard_map/reduce_scatter | solution.py:66
Sparse Core Ops, SparseCore 0:
  9.1 117.3 all-gather.1
  155.4 97.3 reduce-scatter.3
where the time goes:
time: 261 us; the launch traced here: 260 us
  waiting for transfers between devices  177 us (68%)
  local copies, waits for them, and re-layouts  34.7 us (13%)
  matrix products  23.7 us (9%)
  between operations  13.5 us (5%)
  starting transfers between devices  8.86 us (3%)
    reduce_scatter x1, waiting for transfers between devices, body(): lax.psum_scatter(partial_sums, 'row', scatter_dimension=0, tiled=True)  97.5 us
    all_to_all x1, waiting for transfers between devices, body(): lax.all_to_all(outgoing, 'row', split_axis=0, concat_axis=0, tiled=True)  48.2 us
    all_gather x1, waiting for transfers between devices, body(): coeff_piece = lax.all_gather(coeffs, 'col', axis=1, tiled=True)  30.9 us
    dot_general x1, matrix products, product(): lax.dot_general(coeff_piece, kept_rows, (((0,), (0,)), ((), ())), preferr...  16.8 us
    unnamed x3, local copies, waits for them, and re-layouts  12 us
    all_to_all x1, starting transfers between devices, body(): lax.all_to_all(outgoing, 'row', split_axis=0, concat_axis=0, tiled=True)  8.64 us
    reshape x1, local copies, waits for them, and re-layouts, body(): incoming.reshape(slot_count, atom_w * row_width)  7.23 us
    dot_general x1, local copies, waits for them, and re-layouts, body(): jnp.dot(placing, integrals.reshape(per_dev, atom_w * row_width), preferre...  6.28 us
  transfers between devices with their start and end apart: 3, of which 3 were waited for; matrix products, arithmetic and copies ran while one was open for 12% of the time, Pallas kernels for 0%

commit v1 on v0

v1 whole, which is shorter than its diff:
```python
import functools

import jax
import jax.numpy as jnp
from jax import lax
from jax.experimental import pallas as pl
from jax.experimental.pallas import tpu as pltpu
from jax.sharding import PartitionSpec as P

MESH = pl.DeviceIdType.MESH
BF = jnp.bfloat16
F32 = jnp.float32

ROUNDS = 8
LAG = 2.0
AHEAD = 2
V_READY = 56.0
SLOT_US = 2.85


def hops(p):
    return (4, 3) if p % 2 == 0 else (3, 4)


def build_schedule():
    events = []
    done = [0.0] * ROUNDS
    for p in range(ROUNDS):
        for side in range(2):
            for h in range(1, hops(p)[side] + 1):
                key = 3.5 * p + LAG * (h - 1)
                if h == 1:
                    key -= 3.5 * AHEAD
                events.append((max(key, 0.0) * SLOT_US + 4.0, 0, p, h, side))
                last = 3.5 * p + LAG * h
                done[p] = max(done[p], last * SLOT_US + 4.0)
    events.append((V_READY, 1, 0, 0, 0))
    clock = V_READY + 3.0
    for p in range(ROUNDS):
        clock = max(clock, done[p])
        events.append((clock, 2, p, 0, 0))
        events.append((clock + 2.5, 3, p, 0, 0))
        events.append((clock + 7.0, 4, p, 0, 0))
        events.append((clock + 10.5, 5, p, 0, 0))
        clock += 1.4
    return sorted(events)


def kernel(
    pack_s, unpack_s, sig_s, off_s, coef_hbm, v_hbm, out_ref,
    vin, cin, vsend, vrecv, ct, smat, gath, vord, vc, psend, own, prec, q, rb1, red, rb2,
    load_sem, a_send, a_recv, g_send, g_recv, d_send, d_recv, s_send, s_recv, t_send, t_recv,
):
    row = lax.axis_index("row")
    z = lax.axis_index("col")
    core = lax.rem(row, 2)
    chip = lax.div(row, 2)
    x = lax.rem(chip, 4)
    y = lax.div(chip, 4)
    zr = lax.rem(z + 1, 8)
    zl = lax.rem(z + 7, 8)

    load_c = pltpu.make_async_copy(coef_hbm, cin, load_sem.at[0])
    load_v = pltpu.make_async_copy(v_hbm, vin, load_sem.at[1])
    load_c.start()
    load_v.start()

    barrier = pltpu.get_barrier_semaphore()

    def greet(k, carry):
        peer = lax.rem(row + k, 32)
        pl.semaphore_signal(barrier, inc=1, device_id=(peer, z), device_id_type=MESH)
        return carry

    lax.fori_loop(1, 32, greet, 0)
    for side in (zr, zl):
        pl.semaphore_signal(barrier, inc=1, device_id=(row, side), device_id_type=MESH)

    m = lax.broadcasted_iota(jnp.int32, (48, 512), 0)
    k = lax.broadcasted_iota(jnp.int32, (48, 512), 1)
    for g in range(20):
        length = off_s[2 * g + 1] - off_s[2 * g]
        src = jnp.where(m < length, m, 32 + m - length) + 64 * (g % 8)
        smat[48 * g:48 * g + 48, :] = jnp.where(k == src, 1.0, 0.0).astype(BF)
    smat[960:1024, :] = jnp.zeros((64, 512), BF)

    load_c.wait()
    rho = lax.broadcasted_iota(jnp.int32, (512, 512), 0)
    col = lax.broadcasted_iota(jnp.int32, (512, 512), 1)
    want = (rho & 15) + 16 * (rho >> 6) + 256 * ((rho >> 4) & 1) + 128 * ((rho >> 5) & 1)
    perm = jnp.where(col == want, 1.0, 0.0).astype(BF)
    for b in range(5):
        ct[:, 256 * b:256 * b + 256] = lax.dot_general(
            perm, cin[256 * b:256 * b + 256, :], (((1,), (1,)), ((), ())), preferred_element_type=F32
        ).astype(BF)
    for b, (k0, kw, c0, cw) in enumerate(((0, 512, 0, 384), (512, 512, 384, 384), (1024, 256, 768, 256))):
        piece = lax.dot_general(
            ct[:, k0:k0 + kw], smat[c0:c0 + cw, 0:kw], (((1,), (1,)), ((), ())), preferred_element_type=F32
        ).astype(BF)
        gath[:, z, :, c0:c0 + cw] = piece.reshape(8, 64, cw)

    pl.semaphore_wait(barrier, 33)

    def ring(p, h, side):
        src = lax.rem(z + (8 - (h - 1)), 8) if side == 0 else lax.rem(z + (h - 1), 8)
        return pltpu.make_async_remote_copy(
            src_ref=gath.at[p, src],
            dst_ref=gath.at[p, src],
            send_sem=g_send.at[side, p, h - 1],
            recv_sem=g_recv.at[side, p, h - 1],
            device_id=(row, zr if side == 0 else zl),
            device_id_type=MESH,
        )

    def ring_arrival(p, h, side):
        src = lax.rem(z + (8 - h), 8) if side == 0 else lax.rem(z + h, 8)
        pltpu.make_async_remote_copy(
            src_ref=gath.at[p, src],
            dst_ref=gath.at[p, src],
            send_sem=g_send.at[side, p, h - 1],
            recv_sem=g_recv.at[side, p, h - 1],
            device_id=(row, zr if side == 0 else zl),
            device_id_type=MESH,
        ).wait_recv()

    def exchange(k):
        peer = lax.rem(row + k, 32)
        return pltpu.make_async_remote_copy(
            src_ref=vsend.at[pl.ds(2 * peer, 2)],
            dst_ref=vrecv.at[pl.ds(2 * row, 2)],
            send_sem=a_send.at[peer],
            recv_sem=a_recv.at[row],
            device_id=(peer, z),
            device_id_type=MESH,
        )

    def exchange_arrival(k):
        peer = lax.rem(row + k, 32)
        pltpu.make_async_remote_copy(
            src_ref=vsend.at[pl.ds(2 * peer, 2)],
            dst_ref=vrecv.at[pl.ds(2 * peer, 2)],
            send_sem=a_send.at[peer],
            recv_sem=a_recv.at[peer],
            device_id=(peer, z),
            device_id_type=MESH,
        ).wait_recv()

    def pack_and_send():
        load_v.wait()

        def step(k, carry):
            peer = lax.rem(row + k, 32)
            for s in range(2):
                vsend[2 * peer + s] = vin[pack_s[2 * peer + s]]
            exchange(k).start()
            return carry

        lax.fori_loop(1, 32, step, 0)
        for s in range(2):
            vrecv[2 * row + s] = vin[pack_s[2 * row + s]]

    def receive_blocks():
        def wait_one(k, carry):
            exchange_arrival(k)
            return carry

        lax.fori_loop(1, 32, wait_one, 0)

        def place(a, carry):
            live = jnp.full((32, 1024), sig_s[a], jnp.int32).astype(F32).astype(BF)
            vord[pl.ds(pl.multiple_of(32 * a, 32), 32), :] = vrecv[unpack_s[a]] * live
            return carry

        lax.fori_loop(0, 40, place, 0)
        for k0, kw, c0, cw in ((0, 512, 0, 384), (512, 512, 384, 384), (1024, 256, 768, 256)):
            for n in range(4):
                vc[c0:c0 + cw, 256 * n:256 * n + 256] = jnp.dot(
                    smat[c0:c0 + cw, 0:kw], vord[k0:k0 + kw, 256 * n:256 * n + 256], preferred_element_type=F32
                ).astype(BF)

    partner = row + 1 - 2 * core

    def pair_copy(p):
        return pltpu.make_async_remote_copy(
            src_ref=psend.at[p],
            dst_ref=prec.at[p],
            send_sem=d_send.at[p],
            recv_sem=d_recv.at[p],
            device_id=(partner, z),
            device_id_type=MESH,
        )

    def multiply(p):
        theirs = pl.multiple_of(32 * (1 - core), 32)
        mine = pl.multiple_of(32 * core, 32)
        lhs = gath[p, :, pl.ds(theirs, 32), :].reshape(256, 1024)

        for n in range(4):
            psend[p, :, 256 * n:256 * n + 256] = jnp.dot(
                lhs, vc[:, 256 * n:256 * n + 256], preferred_element_type=F32
            ).astype(BF)
        pair_copy(p).start()
        lhs2 = gath[p, :, pl.ds(mine, 32), :].reshape(256, 1024)
        for n in range(4):
            own[p, :, 256 * n:256 * n + 256] = jnp.dot(
                lhs2, vc[:, 256 * n:256 * n + 256], preferred_element_type=F32
            )

    def row_of(yy, xx):
        return (yy * 4 + xx) * 2 + core

    def first_copy(p, half, d):
        if half == 0:
            to = lax.rem(y + d, 4)
            src, dev = q.at[p, to, :, :, 0:512], row_of(to, x)
        else:
            to = lax.rem(x + d, 4)
            src, dev = q.at[p, :, to, :, 512:1024], row_of(y, to)
        return pltpu.make_async_remote_copy(
            src_ref=src,
            dst_ref=rb1.at[p, half, d - 1],
            send_sem=s_send.at[p, half, d - 1],
            recv_sem=s_recv.at[p, half, d - 1],
            device_id=(dev, z),
            device_id_type=MESH,
        )

    def second_copy(p, half, d):
        if half == 0:
            to = lax.rem(x + d, 4)
            dev = row_of(y, to)
        else:
            to = lax.rem(y + d, 4)
            dev = row_of(to, x)
        return pltpu.make_async_remote_copy(
            src_ref=red.at[p, half, to],
            dst_ref=rb2.at[p, half, d - 1],
            send_sem=t_send.at[p, half, d - 1],
            recv_sem=t_recv.at[p, half, d - 1],
            device_id=(dev, z),
            device_id_type=MESH,
        )

    def pair_sum(p):
        pair_copy(p).wait_recv()
        q[p] = (own[p] + prec[p].astype(F32)).astype(BF).reshape(4, 4, 16, 1024)
        for d in (2, 1, 3):
            for half in range(2):
                first_copy(p, half, d).start()

    def first_sum(p):
        for d in (1, 3, 2):
            for half in range(2):
                first_copy(p, half, d).wait_recv()
        for half in range(2):
            mine = q[p, y, :, :, 0:512] if half == 0 else q[p, :, x, :, 512:1024]
            total = mine.astype(F32)
            for d in range(3):
                total = total + rb1[p, half, d].astype(F32)
            red[p, half] = total.astype(BF)
        for d in (2, 1, 3):
            for half in range(2):
                second_copy(p, half, d).start()

    def second_sum(p):
        for d in (1, 3, 2):
            for half in range(2):
                second_copy(p, half, d).wait_recv()
        for half in range(2):
            total = red[p, half, x if half == 0 else y].astype(F32)
            for d in range(3):
                total = total + rb2[p, half, d].astype(F32)
            out_ref[16 * p:16 * p + 16, 512 * half:512 * half + 512] = total.astype(BF)

    packed = False
    for when, kind, p, h, side in build_schedule():
        if kind == 0:
            if h > 1:
                if not packed:
                    pack_and_send()
                    packed = True
                ring_arrival(p, h - 1, side)
            ring(p, h, side).start()
        elif kind == 1:
            receive_blocks()
        elif kind == 2:
            for s in range(2):
                ring_arrival(p, hops(p)[s], s)
            multiply(p)
        elif kind == 3:
            pair_sum(p)
        elif kind == 4:
            first_sum(p)
        else:
            second_sum(p)

    def sent(k, carry):
        exchange(k).wait_send()
        return carry

    lax.fori_loop(1, 32, sent, 0)
    for p in range(ROUNDS):
        for side in range(2):
            for h in range(1, hops(p)[side] + 1):
                ring(p, h, side).wait_send()
        pair_copy(p).wait_send()
        for d in (1, 2, 3):
            for half in range(2):
                first_copy(p, half, d).wait_send()
                second_copy(p, half, d).wait_send()


def body(integrals, coeffs, mask, offsets, atom_of_slot):
    me = lax.axis_index("row")
    col = lax.axis_index("col")
    holders = atom_of_slot.reshape(32, 40)
    counter = jnp.arange(40, dtype=jnp.int32)
    target = lax.dynamic_slice_in_dim(atom_of_slot, me * 40, 40) // 40
    rank = jnp.sum(((target[None, :] == target[:, None]) & (counter[None, :] < counter[:, None])).astype(jnp.int32), axis=1)
    slot = jnp.arange(64, dtype=jnp.int32)
    pack = jnp.sum(jnp.where((2 * target + rank)[None, :] == slot[:, None], counter[None, :], 0), axis=1)
    mine = holders // 40 == me
    arrival = jnp.cumsum(mine.astype(jnp.int32), axis=1) - 1
    place = 2 * jnp.arange(32, dtype=jnp.int32)[:, None] + arrival
    local = jnp.where(mine, holders - me * 40, -1)
    unpack = jnp.sum(jnp.where(local[None] == counter[:, None, None], place[None], 0), axis=(1, 2))
    sig = (lax.dynamic_slice(mask, (me * 40, col), (40, 1))[:, 0] > 0).astype(jnp.int32)
    off = lax.dynamic_slice_in_dim(offsets, me * 40, 41)

    smem = pl.BlockSpec(memory_space=pltpu.SMEM)
    hbm = pl.BlockSpec(memory_space=pl.ANY)
    vmem = pltpu.VMEM
    dma = pltpu.SemaphoreType.DMA
    return pl.pallas_call(
        kernel,
        out_shape=jax.ShapeDtypeStruct((128, 1024), BF),
        in_specs=[smem, smem, smem, smem, hbm, hbm],
        out_specs=pl.BlockSpec(memory_space=pltpu.VMEM),
        scratch_shapes=[
            vmem((40, 32, 1024), BF),
            vmem((1280, 512), BF),
            vmem((64, 32, 1024), BF),
            vmem((64, 32, 1024), BF),
            vmem((512, 1280), BF),
            vmem((1024, 512), BF),
            vmem((ROUNDS, 8, 64, 1024), BF),
            vmem((1280, 1024), BF),
            vmem((1024, 1024), BF),
            vmem((ROUNDS, 256, 1024), BF),
            vmem((ROUNDS, 256, 1024), F32),
            vmem((ROUNDS, 256, 1024), BF),
            vmem((ROUNDS, 4, 4, 16, 1024), BF),
            vmem((ROUNDS, 2, 3, 4, 16, 512), BF),
            vmem((ROUNDS, 2, 4, 16, 512), BF),
            vmem((ROUNDS, 2, 3, 16, 512), BF),
            dma((2,)),
            dma((32,)),
            dma((32,)),
            dma((2, ROUNDS, 4)),
            dma((2, ROUNDS, 4)),
            dma((ROUNDS,)),
            dma((ROUNDS,)),
            dma((ROUNDS, 2, 3)),
            dma((ROUNDS, 2, 3)),
            dma((ROUNDS, 2, 3)),
            dma((ROUNDS, 2, 3)),
        ],
        compiler_params=pltpu.CompilerParams(
            collective_id=0, has_side_effects=True, vmem_limit_bytes=66_000_000
        ),
    )(pack, unpack, sig, off, coeffs, integrals)


def solution(mesh):
    in_specs = (P("row", None, "col"), P("row", "col"), P(), P(), P())
    return jax.shard_map(body, mesh=mesh, in_specs=in_specs, out_specs=P("row", "col"), check_vma=False)
```

time: 261 us -> 152 us (0.58)
  waiting for transfers between devices: 177 us -> 0 us
  Pallas kernels: 0 us -> 141 us
  local copies, waits for them, and re-layouts: 34.7 us -> 3.17 us
  matrix products: 23.7 us -> 0 us
  between operations: 13.5 us -> 0.05 us
  starting transfers between devices: 8.86 us -> 0 us
  other arithmetic: 1.52 us -> 6.76 us
    pallas_call x0 -> x1, Pallas kernels: none -> 141 us  [body(): pl.pallas_call(kernel, out_shape=jax.ShapeDtypeStruct((128, 1024), BF), i...]
    reduce_scatter x1 -> x0, waiting for transfers between devices: 97.5 us -> none  [body(): lax.psum_scatter(partial_sums, 'row', scatter_dimension=0, tiled=True)]
    all_to_all x1 -> x0, waiting for transfers between devices: 48.2 us -> none  [body(): lax.all_to_all(outgoing, 'row', split_axis=0, concat_axis=0, tiled=True)]
    all_gather x1 -> x0, waiting for transfers between devices: 30.9 us -> none  [body(): coeff_piece = lax.all_gather(coeffs, 'col', axis=1, tiled=True)]
    dot_general x3 -> x0, matrix products: 23.7 us -> none  [the longest x1 16.8 us: product(): lax.dot_general(coeff_piece, kept_rows, (((0,), (0,)), ((), ())), preferr...]
    reshape x2 -> x0, local copies, waits for them, and re-layouts: 12.5 us -> none  [the longest x1 7.23 us: body(): incoming.reshape(slot_count, atom_w * row_width)]
    unnamed x3 -> x1, local copies, waits for them, and re-layouts: 12 us -> 1.67 us
    all_to_all x1 -> x0, starting transfers between devices: 8.64 us -> none  [body(): lax.all_to_all(outgoing, 'row', split_axis=0, concat_axis=0, tiled=True)]
  transfers between devices with their start and end apart: 3 -> 0, of which waited for: 3 -> 0; matrix products, arithmetic and copies ran while one was open for 12% -> 0% of each run, Pallas kernels for 0% -> 0%
where the time goes in v1:
time: 152 us; the launch traced here: 151 us
  Pallas kernels  141 us (93%)
  other arithmetic  6.76 us (4%)
  local copies, waits for them, and re-layouts  3.17 us (2%)
    pallas_call x1, Pallas kernels, body(): pl.pallas_call(kernel, out_shape=jax.ShapeDtypeStruct((128, 1024), BF), i...  141 us

profile of v1, /device:TPU:1, one launch (start us, length us, event | category | flops | bytes accessed | tf_op | source)
XLA Modules:
  0.0 150.5 jit_solution(18166897981931618899)
XLA Ops:
  0.0 1.2 dynamic_slice.11.off_s
  1.2 1.3 fusion.3.sig_s
  2.6 0.8 and_select_fusion
  3.3 0.2 convert_reduce_fusion
  3.5 0.8 multiply_add_fusion
  4.3 0.6 select_reduce_fusion.1.pack_s
  4.9 0.7 fusion.2
  5.6 0.1 and.27
  5.7 0.7 broadcast_divide_fusion
  6.4 0.1 div.25
  6.5 0.1 sub.33
  6.6 0.2 reduce_window_sum.11
  6.8 0.1 add_add_fusion
  6.9 1.4 select_reduce_fusion.unpack_s
  8.3 140.6 %shard_map.55 = bf16[128,1024]{1,0:T(8,128)(2,1)} custom-call(s32[64]{0:T(128)} %select_reduce_fusion.1.pack_s, s32[40]{0:T(128)} %select_reduce_fusion.unpack_s, s32[40]{0:T(128)} %fusion.3.sig_s, s32[41]{0:T(128)} %dynamic_slice.11.off_s, bf16[1280,512]{1,0:T(8,128)(2,1)} %coef_hbm.1, bf16[40,32,1024]{2,1,0:T(8,128)(2,1)} %v_hbm.1), custom_call_target="tpu_custom_call" | custom-call | tf_op jit(solution)/shard_map/pallas_call | solution.py:334
  148.9 1.7 %copy.7 = bf16[128,1024]{1,0:T(8,128)(2,1)} copy(bf16[128,1024]{1,0:T(8,128)(2,1)} %shard_map.55) | data formatting | bytes 524288
  (3 shorter events, 0.0 us)

commit v2 on v1

--- a/solution.py
+++ b/solution.py
@@ -14,8 +14,10 @@
 ROUNDS = 8
 LAG = 2.0
 AHEAD = 2
-V_READY = 56.0
-SLOT_US = 2.85
+V_READY = 70.0
+SLOT_US = 2.8
+START = 4.0
+FAR = ((2, 2), (2, 0), (0, 2), (3, 2), (1, 2), (2, 3), (2, 1), (3, 1), (3, 3), (1, 3), (1, 1), (3, 0), (0, 3), (1, 0), (0, 1))
 
 
 def hops(p):
@@ -31,9 +33,9 @@
                 key = 3.5 * p + LAG * (h - 1)
                 if h == 1:
                     key -= 3.5 * AHEAD
-                events.append((max(key, 0.0) * SLOT_US + 4.0, 0, p, h, side))
+                events.append((max(key, 0.0) * SLOT_US + START, 0, p, h, side))
                 last = 3.5 * p + LAG * h
-                done[p] = max(done[p], last * SLOT_US + 4.0)
+                done[p] = max(done[p], last * SLOT_US + START)
     events.append((V_READY, 1, 0, 0, 0))
     clock = V_READY + 3.0
     for p in range(ROUNDS):
@@ -47,8 +49,9 @@
 
 
 def kernel(
-    pack_s, unpack_s, sig_s, off_s, coef_hbm, v_hbm, out_ref,
-    vin, cin, vsend, vrecv, ct, smat, gath, vord, vc, psend, own, prec, q, rb1, red, rb2,
+    off_s, holder_hbm, mask_hbm, coef_hbm, v_hbm, out_ref,
+    holder, mask, table, table_s,
+    vin, cin, vsend, vrecv, ct, smat, gath, vord, vc, vtail, psend, own, prec, q, rb1, red, rb2,
     load_sem, a_send, a_recv, g_send, g_recv, d_send, d_recv, s_send, s_recv, t_send, t_recv,
 ):
     row = lax.axis_index("row")
@@ -63,6 +66,10 @@
     load_c = pltpu.make_async_copy(coef_hbm, cin, load_sem.at[0])
     load_v = pltpu.make_async_copy(v_hbm, vin, load_sem.at[1])
     load_c.start()
+    load_h = pltpu.make_async_copy(holder_hbm, holder, load_sem.at[2])
+    load_m = pltpu.make_async_copy(mask_hbm, mask, load_sem.at[3])
+    load_h.start()
+    load_m.start()
     load_v.start()
 
     barrier = pltpu.get_barrier_semaphore()
@@ -79,25 +86,42 @@
     m = lax.broadcasted_iota(jnp.int32, (48, 512), 0)
     k = lax.broadcasted_iota(jnp.int32, (48, 512), 1)
     for g in range(20):
-        length = off_s[2 * g + 1] - off_s[2 * g]
+        at = row * 40 + 2 * g
+        length = off_s[at + 1] - off_s[at]
         src = jnp.where(m < length, m, 32 + m - length) + 64 * (g % 8)
-        smat[48 * g:48 * g + 48, :] = jnp.where(k == src, 1.0, 0.0).astype(BF)
-    smat[960:1024, :] = jnp.zeros((64, 512), BF)
+        rows = jnp.where(k == src, 1.0, 0.0).astype(BF)
+        if g < 18:
+            smat[48 * g:48 * g + 48, :] = rows
+        elif g == 18:
+            smat[864:896, :] = rows[0:32]
+            smat[960:976, :] = rows[32:48]
+        else:
+            smat[976:1024, :] = rows
+    smat[896:960, :] = jnp.zeros((64, 512), BF)
+    smat[1024:1088, :] = jnp.zeros((64, 512), BF)
 
     load_c.wait()
     rho = lax.broadcasted_iota(jnp.int32, (512, 512), 0)
     col = lax.broadcasted_iota(jnp.int32, (512, 512), 1)
-    want = (rho & 15) + 16 * (rho >> 6) + 256 * ((rho >> 4) & 1) + 128 * ((rho >> 5) & 1)
+    want = (rho & 15) + 256 * ((rho >> 4) & 1) + 16 * ((rho >> 5) & 7) + 128 * (rho >> 8)
     perm = jnp.where(col == want, 1.0, 0.0).astype(BF)
     for b in range(5):
         ct[:, 256 * b:256 * b + 256] = lax.dot_general(
             perm, cin[256 * b:256 * b + 256, :], (((1,), (1,)), ((), ())), preferred_element_type=F32
         ).astype(BF)
-    for b, (k0, kw, c0, cw) in enumerate(((0, 512, 0, 384), (512, 512, 384, 384), (1024, 256, 768, 256))):
-        piece = lax.dot_general(
-            ct[:, k0:k0 + kw], smat[c0:c0 + cw, 0:kw], (((1,), (1,)), ((), ())), preferred_element_type=F32
-        ).astype(BF)
-        gath[:, z, :, c0:c0 + cw] = piece.reshape(8, 64, cw)
+
+    def compact(r0, rw, k0, kw, c0, cw):
+        return lax.dot_general(
+            ct[r0:r0 + rw, k0:k0 + kw], smat[c0:c0 + cw, 0:kw], (((1,), (1,)), ((), ())), preferred_element_type=F32
+        )
+
+    for t0, k0, kw, c0, cw in ((0, 0, 512, 0, 384), (3, 512, 512, 384, 384), (6, 1024, 256, 768, 128)):
+        piece = compact(0, 512, k0, kw, c0, cw).astype(BF).reshape(2, 8, 32, cw)
+        for qc in range(2):
+            for t in range(cw // 128):
+                gath[:, z, 7 * qc + t0 + t] = piece[qc, :, :, 128 * t:128 * t + 128]
+    tail = compact(0, 256, 1024, 256, 960, 128) + compact(256, 256, 1024, 256, 896, 128)
+    gath[:, z, 14] = tail.astype(BF).reshape(8, 32, 128)
 
     pl.semaphore_wait(barrier, 33)
 
@@ -123,8 +147,15 @@
             device_id_type=MESH,
         ).wait_recv()
 
+    def peer_of(k):
+        if k == 30:
+            return row + 1 - 2 * core
+        dy, dx = FAR[k // 2]
+        other = core if k % 2 == 0 else 1 - core
+        return (lax.rem(y + dy, 4) * 4 + lax.rem(x + dx, 4)) * 2 + other
+
     def exchange(k):
-        peer = lax.rem(row + k, 32)
+        peer = peer_of(k)
         return pltpu.make_async_remote_copy(
             src_ref=vsend.at[pl.ds(2 * peer, 2)],
             dst_ref=vrecv.at[pl.ds(2 * row, 2)],
@@ -145,19 +176,41 @@
             device_id_type=MESH,
         ).wait_recv()
 
+    def build_tables():
+        load_h.wait()
+        load_m.wait()
+        lane = lax.broadcasted_iota(jnp.int32, (40, 1280), 1)
+        atom = lax.broadcasted_iota(jnp.int32, (40, 1280), 0)
+        held = jnp.broadcast_to(holder[...], (40, 1280))
+        owner = lax.shift_right_logical(held * 52429, 21)
+        slot = jnp.max(jnp.where(held == atom + 40 * row, lane, 0), axis=1, keepdims=True)
+        source = lax.shift_right_logical(slot * 52429, 21)
+        earlier = (owner == row) & (lane >= 40 * source) & (lane < slot)
+        arrive = 2 * source + jnp.max(jnp.where(earlier, 1, 0), axis=1, keepdims=True)
+        wanted = jnp.broadcast_to(mask[pl.ds(z, 1), :], (40, 1280))
+        live = jnp.sum(jnp.where(lane == atom + 40 * row, wanted, 0), axis=1, keepdims=True)
+        place = lane - 40 * row
+        here = (owner == atom) & (place >= 0) & (place < 40)
+        first = jnp.min(jnp.where(here, place, 39), axis=1, keepdims=True)
+        last = jnp.max(jnp.where(here, place, 0), axis=1, keepdims=True)
+        diagonal = lax.broadcasted_iota(jnp.int32, (40, 128), 1) == lax.broadcasted_iota(jnp.int32, (40, 128), 0)
+        for r, value in enumerate((arrive, live, first, last)):
+            table[r:r + 1, :] = jnp.sum(jnp.where(diagonal, value, 0), axis=0, keepdims=True)
+        table[4:8, :] = jnp.zeros((4, 128), jnp.int32)
+        to_scalar = pltpu.make_async_copy(table, table_s, load_sem.at[4])
+        to_scalar.start()
+        to_scalar.wait()
+
     def pack_and_send():
+        build_tables()
         load_v.wait()
-
-        def step(k, carry):
-            peer = lax.rem(row + k, 32)
+        for k in range(31):
+            peer = peer_of(k)
             for s in range(2):
-                vsend[2 * peer + s] = vin[pack_s[2 * peer + s]]
+                vsend[2 * peer + s] = vin[table_s[2 + s, peer]]
             exchange(k).start()
-            return carry
-
-        lax.fori_loop(1, 32, step, 0)
         for s in range(2):
-            vrecv[2 * row + s] = vin[pack_s[2 * row + s]]
+            vrecv[2 * row + s] = vin[table_s[2 + s, row]]
 
     def receive_blocks():
         def wait_one(k, carry):
@@ -167,16 +220,17 @@
         lax.fori_loop(1, 32, wait_one, 0)
 
         def place(a, carry):
-            live = jnp.full((32, 1024), sig_s[a], jnp.int32).astype(F32).astype(BF)
-            vord[pl.ds(pl.multiple_of(32 * a, 32), 32), :] = vrecv[unpack_s[a]] * live
+            live = jnp.full((32, 1024), table_s[1, a], jnp.int32).astype(F32).astype(BF)
+            vord[pl.ds(pl.multiple_of(32 * a, 32), 32), :] = vrecv[table_s[0, a]] * live
             return carry
 
         lax.fori_loop(0, 40, place, 0)
-        for k0, kw, c0, cw in ((0, 512, 0, 384), (512, 512, 384, 384), (1024, 256, 768, 256)):
+        for k0, kw, c0, cw in ((0, 512, 0, 384), (512, 512, 384, 384), (1024, 256, 768, 128)):
             for n in range(4):
                 vc[c0:c0 + cw, 256 * n:256 * n + 256] = jnp.dot(
                     smat[c0:c0 + cw, 0:kw], vord[k0:k0 + kw, 256 * n:256 * n + 256], preferred_element_type=F32
                 ).astype(BF)
+        vtail[...] = jnp.dot(smat[896:1088, 0:256], vord[1024:1280, :], preferred_element_type=F32).astype(BF)
 
     partner = row + 1 - 2 * core
 
@@ -190,21 +244,20 @@
             device_id_type=MESH,
         )
 
+    def product(p, qc, n):
+        tiles = [gath[p, :, 7 * qc + t].reshape(256, 128) for t in range(7)] + [gath[p, :, 14].reshape(256, 128)]
+        start = pl.multiple_of(64 * (1 - qc), 64)
+        rhs = jnp.concatenate(
+            [vc[:, 256 * n:256 * n + 256], vtail[pl.ds(start, 128), 256 * n:256 * n + 256]], axis=0
+        )
+        return jnp.dot(jnp.concatenate(tiles, axis=1), rhs, preferred_element_type=F32)
+
     def multiply(p):
-        theirs = pl.multiple_of(32 * (1 - core), 32)
-        mine = pl.multiple_of(32 * core, 32)
-        lhs = gath[p, :, pl.ds(theirs, 32), :].reshape(256, 1024)
-
         for n in range(4):
-            psend[p, :, 256 * n:256 * n + 256] = jnp.dot(
-                lhs, vc[:, 256 * n:256 * n + 256], preferred_element_type=F32
-            ).astype(BF)
+            psend[p, :, 256 * n:256 * n + 256] = product(p, 1 - core, n).astype(BF)
         pair_copy(p).start()
-        lhs2 = gath[p, :, pl.ds(mine, 32), :].reshape(256, 1024)
         for n in range(4):
-            own[p, :, 256 * n:256 * n + 256] = jnp.dot(
-                lhs2, vc[:, 256 * n:256 * n + 256], preferred_element_type=F32
-            )
+            own[p, :, 256 * n:256 * n + 256] = product(p, core, n)
 
     def row_of(yy, xx):
         return (yy * 4 + xx) * 2 + core
@@ -294,11 +347,8 @@
         else:
             second_sum(p)
 
-    def sent(k, carry):
+    for k in range(31):
         exchange(k).wait_send()
-        return carry
-
-    lax.fori_loop(1, 32, sent, 0)
     for p in range(ROUNDS):
         for side in range(2):
             for h in range(1, hops(p)[side] + 1):
@@ -311,22 +361,6 @@
 
 
 def body(integrals, coeffs, mask, offsets, atom_of_slot):
-    me = lax.axis_index("row")
-    col = lax.axis_index("col")
-    holders = atom_of_slot.reshape(32, 40)
-    counter = jnp.arange(40, dtype=jnp.int32)
-    target = lax.dynamic_slice_in_dim(atom_of_slot, me * 40, 40) // 40
-    rank = jnp.sum(((target[None, :] == target[:, None]) & (counter[None, :] < counter[:, None])).astype(jnp.int32), axis=1)
-    slot = jnp.arange(64, dtype=jnp.int32)
-    pack = jnp.sum(jnp.where((2 * target + rank)[None, :] == slot[:, None], counter[None, :], 0), axis=1)
-    mine = holders // 40 == me
-    arrival = jnp.cumsum(mine.astype(jnp.int32), axis=1) - 1
-    place = 2 * jnp.arange(32, dtype=jnp.int32)[:, None] + arrival
-    local = jnp.where(mine, holders - me * 40, -1)
-    unpack = jnp.sum(jnp.where(local[None] == counter[:, None, None], place[None], 0), axis=(1, 2))
-    sig = (lax.dynamic_slice(mask, (me * 40, col), (40, 1))[:, 0] > 0).astype(jnp.int32)
-    off = lax.dynamic_slice_in_dim(offsets, me * 40, 41)
-
     smem = pl.BlockSpec(memory_space=pltpu.SMEM)
     hbm = pl.BlockSpec(memory_space=pl.ANY)
     vmem = pltpu.VMEM
@@ -334,18 +368,23 @@
     return pl.pallas_call(
         kernel,
         out_shape=jax.ShapeDtypeStruct((128, 1024), BF),
-        in_specs=[smem, smem, smem, smem, hbm, hbm],
+        in_specs=[smem, hbm, hbm, hbm, hbm],
         out_specs=pl.BlockSpec(memory_space=pltpu.VMEM),
         scratch_shapes=[
+            vmem((1, 1280), jnp.int32),
+            vmem((8, 1280), jnp.int32),
+            vmem((8, 128), jnp.int32),
+            pltpu.SMEM((8, 128), jnp.int32),
             vmem((40, 32, 1024), BF),
             vmem((1280, 512), BF),
             vmem((64, 32, 1024), BF),
             vmem((64, 32, 1024), BF),
             vmem((512, 1280), BF),
-            vmem((1024, 512), BF),
-            vmem((ROUNDS, 8, 64, 1024), BF),
+            vmem((1088, 512), BF),
+            vmem((ROUNDS, 8, 15, 32, 128), BF),
             vmem((1280, 1024), BF),
-            vmem((1024, 1024), BF),
+            vmem((896, 1024), BF),
+            vmem((192, 1024), BF),
             vmem((ROUNDS, 256, 1024), BF),
             vmem((ROUNDS, 256, 1024), F32),
             vmem((ROUNDS, 256, 1024), BF),
@@ -353,7 +392,7 @@
             vmem((ROUNDS, 2, 3, 4, 16, 512), BF),
             vmem((ROUNDS, 2, 4, 16, 512), BF),
             vmem((ROUNDS, 2, 3, 16, 512), BF),
-            dma((2,)),
+            dma((5,)),
             dma((32,)),
             dma((32,)),
             dma((2, ROUNDS, 4)),
@@ -368,7 +407,7 @@
         compiler_params=pltpu.CompilerParams(
             collective_id=0, has_side_effects=True, vmem_limit_bytes=66_000_000
         ),
-    )(pack, unpack, sig, off, coeffs, integrals)
+    )(offsets, atom_of_slot.reshape(1, 1280), mask.T, coeffs, integrals)
 
 
 def solution(mesh):

time: 152 us -> 125 us (0.82)
  Pallas kernels: 141 us -> 122 us
  other arithmetic: 6.76 us -> 0 us
    pallas_call x1, Pallas kernels: 141 us -> 122 us  [body(): pl.pallas_call(kernel, out_shape=jax.ShapeDtypeStruct((128, 1024), BF), i...]
    reduce_sum x3 -> x0, other arithmetic: 2.18 us -> none  [the longest x1 1.4 us: body(): jnp.sum(jnp.where(local[None] == counter[:, None, None], place[None], 0),...]
where the time goes in v2:
time: 125 us
  Pallas kernels  122 us (98%)
  local copies, waits for them, and re-layouts  2.96 us (2%)
    pallas_call x1, Pallas kernels, body(): pl.pallas_call(kernel, out_shape=jax.ShapeDtypeStruct((128, 1024), BF), i...  122 us

profile of v2, /device:TPU:1, one launch (start us, length us, event | category | flops | bytes accessed | tf_op | source)
XLA Modules:
  0.0 124.6 jit_solution(14935688284434394406)
XLA Ops:
  0.0 1.3 %reshape.3.holder_hbm = s32[1,1280]{1,0:T(1,128)} reshape(s32[1280]{0:T(1024)} %param.9) | data formatting | bytes 10240 | tf_op jit(solution)/shard_map/reshape | solution.py:410
  1.3 121.6 %shard_map.55 = bf16[128,1024]{1,0:T(8,128)(2,1)} custom-call(s32[1281]{0:T(1024)} %off_s.1, s32[1,1280]{1,0:T(1,128)} %reshape.3.holder_hbm, s32[8,1280]{1,0:T(8,128)} %bitcast.1, bf16[1280,512]{1,0:T(8,128)(2,1)} %coef_hbm.1, bf16[40,32,1024]{2,1,0:T(8,128)(2,1)} %v_hbm.1), custom_call_target="tpu_custom_call" | custom-call | tf_op jit(solution)/shard_map/pallas_call | solution.py:368
  122.9 1.7 %copy.7 = bf16[128,1024]{1,0:T(8,128)(2,1)} copy(bf16[128,1024]{1,0:T(8,128)(2,1)} %shard_map.55) | data formatting | bytes 524288

commit v3 on v2

--- a/solution.py
+++ b/solution.py
@@ -12,47 +12,82 @@
 F32 = jnp.float32
 
 ROUNDS = 8
-LAG = 2.0
-AHEAD = 2
-V_READY = 70.0
-SLOT_US = 2.8
-START = 4.0
 FAR = ((2, 2), (2, 0), (0, 2), (3, 2), (1, 2), (2, 3), (2, 1), (3, 1), (3, 3), (1, 3), (1, 1), (3, 0), (0, 3), (1, 0), (0, 1))
 
+START = 5.0
+SLOT = 2.68
+WIRE = 2.4
+V_READY = 59.0
+LAG = 2
+
 
 def hops(p):
-    return (4, 3) if p % 2 == 0 else (3, 4)
+    return (4, 3) if p % 4 < 2 else (3, 4)
+
+
+RING_SEM = {
+    key: n
+    for n, key in enumerate(
+        (side, p, h) for p in range(ROUNDS) for side in range(2) for h in range(1, hops(p)[side] + 1)
+    )
+}
+
+
+def ring_slots(side):
+    slot_of = {}
+    slot = 0
+    while len(slot_of) < sum(hops(p)[side] for p in range(ROUNDS)):
+        for p in range(ROUNDS):
+            h = 1
+            while (p, h) in slot_of:
+                h += 1
+            if h <= hops(p)[side] and (h == 1 or slot_of[p, h - 1] + LAG <= slot):
+                slot_of[p, h] = slot
+                break
+        slot += 1
+    return slot_of
 
 
 def build_schedule():
-    events = []
-    done = [0.0] * ROUNDS
-    for p in range(ROUNDS):
-        for side in range(2):
-            for h in range(1, hops(p)[side] + 1):
-                key = 3.5 * p + LAG * (h - 1)
-                if h == 1:
-                    key -= 3.5 * AHEAD
-                events.append((max(key, 0.0) * SLOT_US + START, 0, p, h, side))
-                last = 3.5 * p + LAG * h
-                done[p] = max(done[p], last * SLOT_US + START)
-    events.append((V_READY, 1, 0, 0, 0))
-    clock = V_READY + 3.0
-    for p in range(ROUNDS):
-        clock = max(clock, done[p])
-        events.append((clock, 2, p, 0, 0))
-        events.append((clock + 2.5, 3, p, 0, 0))
-        events.append((clock + 7.0, 4, p, 0, 0))
-        events.append((clock + 10.5, 5, p, 0, 0))
-        clock += 1.4
-    return sorted(events)
+    slots = [ring_slots(side) for side in range(2)]
+    landed = lambda p, h, side: START + (slots[side][p, h] + 1) * SLOT + WIRE
+    pending = [(V_READY, 1, "blocks", 0, 0, 0)]
+    for side in range(2):
+        for (p, h), slot in slots[side].items():
+            if h == 1:
+                pending.append((START + max(0, slot - 2) * SLOT, 0, "ring", p, h, side))
+            else:
+                pending.append((landed(p, h - 1, side), 0, "ring", p, h, side))
+    order, clock, links = [], START, 0.0
+    have_blocks = False
+    cost = {"ring": 0.02, "blocks": 2.0, "multiply": 1.4, "pair": 0.15, "first": 0.15, "second": 0.05}
+    while pending:
+        clock = max(clock, min(e[0] for e in pending))
+        event = min((e for e in pending if e[0] <= clock), key=lambda e: (e[1], e[3], e[0], e[4]))
+        pending.remove(event)
+        order.append(event[2:])
+        kind, p = event[2:4]
+        clock += cost[kind]
+        if kind == "blocks":
+            for p in range(ROUNDS):
+                ready = max(landed(p, hops(p)[side], side) for side in range(2))
+                pending.append((ready, 3, "multiply", p, 0, 0))
+        elif kind == "multiply":
+            pending.append((clock + 1.0, 2, "pair", p, 0, 0))
+        elif kind == "pair":
+            links = max(links, clock) + 2.75
+            pending.append((links + WIRE, 2, "first", p, 0, 0))
+        elif kind == "first":
+            links = max(links, clock) + 0.7
+            pending.append((links + WIRE, 2, "second", p, 0, 0))
+    return order
 
 
 def kernel(
     off_s, holder_hbm, mask_hbm, coef_hbm, v_hbm, out_ref,
     holder, mask, table, table_s,
     vin, cin, vsend, vrecv, ct, smat, gath, vord, vc, vtail, psend, own, prec, q, rb1, red, rb2,
-    load_sem, a_send, a_recv, g_send, g_recv, d_send, d_recv, s_send, s_recv, t_send, t_recv,
+    load_sem, sent, a_recv, g_recv, d_recv, s_recv, t_recv,
 ):
     row = lax.axis_index("row")
     z = lax.axis_index("col")
@@ -130,8 +165,8 @@
         return pltpu.make_async_remote_copy(
             src_ref=gath.at[p, src],
             dst_ref=gath.at[p, src],
-            send_sem=g_send.at[side, p, h - 1],
-            recv_sem=g_recv.at[side, p, h - 1],
+            send_sem=sent.at[1],
+            recv_sem=g_recv.at[RING_SEM[side, p, h]],
             device_id=(row, zr if side == 0 else zl),
             device_id_type=MESH,
         )
@@ -141,40 +176,38 @@
         pltpu.make_async_remote_copy(
             src_ref=gath.at[p, src],
             dst_ref=gath.at[p, src],
-            send_sem=g_send.at[side, p, h - 1],
-            recv_sem=g_recv.at[side, p, h - 1],
+            send_sem=sent.at[1],
+            recv_sem=g_recv.at[RING_SEM[side, p, h]],
             device_id=(row, zr if side == 0 else zl),
             device_id_type=MESH,
         ).wait_recv()
 
-    def peer_of(k):
+    def place_of(k):
         if k == 30:
             return row + 1 - 2 * core
         dy, dx = FAR[k // 2]
         other = core if k % 2 == 0 else 1 - core
         return (lax.rem(y + dy, 4) * 4 + lax.rem(x + dx, 4)) * 2 + other
 
+    def peer_of(k):
+        return jnp.where(core == 0, place_of(k), place_of(30 - k))
+
     def exchange(k):
         peer = peer_of(k)
         return pltpu.make_async_remote_copy(
             src_ref=vsend.at[pl.ds(2 * peer, 2)],
             dst_ref=vrecv.at[pl.ds(2 * row, 2)],
-            send_sem=a_send.at[peer],
-            recv_sem=a_recv.at[row],
+            send_sem=sent.at[0],
+            recv_sem=a_recv.at[0],
             device_id=(peer, z),
             device_id_type=MESH,
         )
 
-    def exchange_arrival(k):
-        peer = lax.rem(row + k, 32)
-        pltpu.make_async_remote_copy(
-            src_ref=vsend.at[pl.ds(2 * peer, 2)],
-            dst_ref=vrecv.at[pl.ds(2 * peer, 2)],
-            send_sem=a_send.at[peer],
-            recv_sem=a_recv.at[peer],
-            device_id=(peer, z),
-            device_id_type=MESH,
-        ).wait_recv()
+    def all_of(ref, send_sem, recv_sem):
+        return pltpu.make_async_remote_copy(
+            src_ref=ref, dst_ref=ref, send_sem=send_sem, recv_sem=recv_sem,
+            device_id=(row, zr), device_id_type=MESH,
+        )
 
     def build_tables():
         load_h.wait()
@@ -213,11 +246,7 @@
             vrecv[2 * row + s] = vin[table_s[2 + s, row]]
 
     def receive_blocks():
-        def wait_one(k, carry):
-            exchange_arrival(k)
-            return carry
-
-        lax.fori_loop(1, 32, wait_one, 0)
+        all_of(vrecv.at[0:62], sent.at[0], a_recv.at[0]).wait_recv()
 
         def place(a, carry):
             live = jnp.full((32, 1024), table_s[1, a], jnp.int32).astype(F32).astype(BF)
@@ -238,7 +267,7 @@
         return pltpu.make_async_remote_copy(
             src_ref=psend.at[p],
             dst_ref=prec.at[p],
-            send_sem=d_send.at[p],
+            send_sem=sent.at[2],
             recv_sem=d_recv.at[p],
             device_id=(partner, z),
             device_id_type=MESH,
@@ -272,8 +301,8 @@
         return pltpu.make_async_remote_copy(
             src_ref=src,
             dst_ref=rb1.at[p, half, d - 1],
-            send_sem=s_send.at[p, half, d - 1],
-            recv_sem=s_recv.at[p, half, d - 1],
+            send_sem=sent.at[3],
+            recv_sem=s_recv.at[p],
             device_id=(dev, z),
             device_id_type=MESH,
         )
@@ -288,8 +317,8 @@
         return pltpu.make_async_remote_copy(
             src_ref=red.at[p, half, to],
             dst_ref=rb2.at[p, half, d - 1],
-            send_sem=t_send.at[p, half, d - 1],
-            recv_sem=t_recv.at[p, half, d - 1],
+            send_sem=sent.at[4],
+            recv_sem=t_recv.at[p],
             device_id=(dev, z),
             device_id_type=MESH,
         )
@@ -302,9 +331,7 @@
                 first_copy(p, half, d).start()
 
     def first_sum(p):
-        for d in (1, 3, 2):
-            for half in range(2):
-                first_copy(p, half, d).wait_recv()
+        all_of(rb1.at[p], sent.at[3], s_recv.at[p]).wait_recv()
         for half in range(2):
             mine = q[p, y, :, :, 0:512] if half == 0 else q[p, :, x, :, 512:1024]
             total = mine.astype(F32)
@@ -316,9 +343,7 @@
                 second_copy(p, half, d).start()
 
     def second_sum(p):
-        for d in (1, 3, 2):
-            for half in range(2):
-                second_copy(p, half, d).wait_recv()
+        all_of(rb2.at[p], sent.at[4], t_recv.at[p]).wait_recv()
         for half in range(2):
             total = red[p, half, x if half == 0 else y].astype(F32)
             for d in range(3):
@@ -326,38 +351,32 @@
             out_ref[16 * p:16 * p + 16, 512 * half:512 * half + 512] = total.astype(BF)
 
     packed = False
-    for when, kind, p, h, side in build_schedule():
-        if kind == 0:
+    for kind, p, h, side in build_schedule():
+        if kind == "ring":
             if h > 1:
                 if not packed:
                     pack_and_send()
                     packed = True
                 ring_arrival(p, h - 1, side)
             ring(p, h, side).start()
-        elif kind == 1:
+        elif kind == "blocks":
             receive_blocks()
-        elif kind == 2:
+        elif kind == "multiply":
             for s in range(2):
                 ring_arrival(p, hops(p)[s], s)
             multiply(p)
-        elif kind == 3:
+        elif kind == "pair":
             pair_sum(p)
-        elif kind == 4:
+        elif kind == "first":
             first_sum(p)
         else:
             second_sum(p)
 
-    for k in range(31):
-        exchange(k).wait_send()
-    for p in range(ROUNDS):
-        for side in range(2):
-            for h in range(1, hops(p)[side] + 1):
-                ring(p, h, side).wait_send()
-        pair_copy(p).wait_send()
-        for d in (1, 2, 3):
-            for half in range(2):
-                first_copy(p, half, d).wait_send()
-                second_copy(p, half, d).wait_send()
+    all_of(vsend.at[0:62], sent.at[0], a_recv.at[0]).wait_send()
+    all_of(gath.at[0:7], sent.at[1], a_recv.at[0]).wait_send()
+    all_of(psend, sent.at[2], a_recv.at[0]).wait_send()
+    all_of(rb1, sent.at[3], a_recv.at[0]).wait_send()
+    all_of(rb2, sent.at[4], a_recv.at[0]).wait_send()
 
 
 def body(integrals, coeffs, mask, offsets, atom_of_slot):
@@ -393,16 +412,12 @@
             vmem((ROUNDS, 2, 4, 16, 512), BF),
             vmem((ROUNDS, 2, 3, 16, 512), BF),
             dma((5,)),
-            dma((32,)),
-            dma((32,)),
-            dma((2, ROUNDS, 4)),
-            dma((2, ROUNDS, 4)),
+            dma((5,)),
+            dma((1,)),
+            dma((len(RING_SEM),)),
             dma((ROUNDS,)),
             dma((ROUNDS,)),
-            dma((ROUNDS, 2, 3)),
-            dma((ROUNDS, 2, 3)),
-            dma((ROUNDS, 2, 3)),
-            dma((ROUNDS, 2, 3)),
+            dma((ROUNDS,)),
         ],
         compiler_params=pltpu.CompilerParams(
             collective_id=0, has_side_effects=True, vmem_limit_bytes=66_000_000

time: 125 us -> 107 us (0.86)
  Pallas kernels: 122 us -> 104 us
    pallas_call x1, Pallas kernels: 122 us -> 104 us  [body(): pl.pallas_call(kernel, out_shape=jax.ShapeDtypeStruct((128, 1024), BF), i...]
where the time goes in v3:
time: 107 us
  Pallas kernels  104 us (97%)
  local copies, waits for them, and re-layouts  2.96 us (3%)
    pallas_call x1, Pallas kernels, body(): pl.pallas_call(kernel, out_shape=jax.ShapeDtypeStruct((128, 1024), BF), i...  104 us

profile of v3, /device:TPU:1, one launch (start us, length us, event | category | flops | bytes accessed | tf_op | source)
XLA Modules:
  0.0 106.7 jit_solution(3766010952396238197)
XLA Ops:
  0.0 1.3 %reshape.3.holder_hbm = s32[1,1280]{1,0:T(1,128)} reshape(s32[1280]{0:T(1024)} %param.9) | data formatting | bytes 10240 | tf_op jit(solution)/shard_map/reshape | solution.py:425
  1.3 103.8 %shard_map.55 = bf16[128,1024]{1,0:T(8,128)(2,1)} custom-call(s32[1281]{0:T(1024)} %off_s.1, s32[1,1280]{1,0:T(1,128)} %reshape.3.holder_hbm, s32[8,1280]{1,0:T(8,128)} %bitcast.1, bf16[1280,512]{1,0:T(8,128)(2,1)} %coef_hbm.1, bf16[40,32,1024]{2,1,0:T(8,128)(2,1)} %v_hbm.1), custom_call_target="tpu_custom_call" | custom-call | tf_op jit(solution)/shard_map/pallas_call | solution.py:387
  105.1 1.7 %copy.7 = bf16[128,1024]{1,0:T(8,128)(2,1)} copy(bf16[128,1024]{1,0:T(8,128)(2,1)} %shard_map.55) | data formatting | bytes 524288

commit v4 on v3

--- a/solution.py
+++ b/solution.py
@@ -14,10 +14,10 @@
 ROUNDS = 8
 FAR = ((2, 2), (2, 0), (0, 2), (3, 2), (1, 2), (2, 3), (2, 1), (3, 1), (3, 3), (1, 3), (1, 1), (3, 0), (0, 3), (1, 0), (0, 1))
 
-START = 5.0
-SLOT = 2.68
+START = 5.5
+SLOT = 2.65
 WIRE = 2.4
-V_READY = 59.0
+V_READY = 55.5
 LAG = 2
 
 
@@ -60,7 +60,7 @@
                 pending.append((landed(p, h - 1, side), 0, "ring", p, h, side))
     order, clock, links = [], START, 0.0
     have_blocks = False
-    cost = {"ring": 0.02, "blocks": 2.0, "multiply": 1.4, "pair": 0.15, "first": 0.15, "second": 0.05}
+    cost = {"ring": 0.02, "blocks": 0.8, "compact": 0.9, "theirs": 0.72, "mine": 0.7, "pair": 0.15, "first": 0.15, "second": 0.05}
     while pending:
         clock = max(clock, min(e[0] for e in pending))
         event = min((e for e in pending if e[0] <= clock), key=lambda e: (e[1], e[3], e[0], e[4]))
@@ -69,17 +69,21 @@
         kind, p = event[2:4]
         clock += cost[kind]
         if kind == "blocks":
+            pending.append((clock, 3, "compact", -1, 0, 0))
+        elif kind == "compact":
             for p in range(ROUNDS):
                 ready = max(landed(p, hops(p)[side], side) for side in range(2))
-                pending.append((ready, 3, "multiply", p, 0, 0))
-        elif kind == "multiply":
-            pending.append((clock + 1.0, 2, "pair", p, 0, 0))
+                pending.append((ready, 3 if p < ROUNDS - 2 else 1, "theirs", p, 0, 0))
+        elif kind == "theirs":
+            pending.append((clock, 3 if p < ROUNDS - 2 else 1, "mine", p, 0, 0))
+        elif kind == "mine":
+            pending.append((clock + (4.0 if p < ROUNDS - 1 else 1.6), 2, "pair", p, 0, 0))
         elif kind == "pair":
             links = max(links, clock) + 2.75
-            pending.append((links + WIRE, 2, "first", p, 0, 0))
+            pending.append((links + WIRE + 1.0, 2, "first", p, 0, 0))
         elif kind == "first":
             links = max(links, clock) + 0.7
-            pending.append((links + WIRE, 2, "second", p, 0, 0))
+            pending.append((links + WIRE + 0.5, 2, "second", p, 0, 0))
     return order
 
 
@@ -214,7 +218,7 @@
         load_m.wait()
         lane = lax.broadcasted_iota(jnp.int32, (40, 1280), 1)
         atom = lax.broadcasted_iota(jnp.int32, (40, 1280), 0)
-        held = jnp.broadcast_to(holder[...], (40, 1280))
+        held = jnp.concatenate([jnp.broadcast_to(holder[r:r + 1, :], (40, 128)) for r in range(10)], axis=1)
         owner = lax.shift_right_logical(held * 52429, 21)
         slot = jnp.max(jnp.where(held == atom + 40 * row, lane, 0), axis=1, keepdims=True)
         source = lax.shift_right_logical(slot * 52429, 21)
@@ -254,6 +258,8 @@
             return carry
 
         lax.fori_loop(0, 40, place, 0)
+
+    def compact_blocks():
         for k0, kw, c0, cw in ((0, 512, 0, 384), (512, 512, 384, 384), (1024, 256, 768, 128)):
             for n in range(4):
                 vc[c0:c0 + cw, 256 * n:256 * n + 256] = jnp.dot(
@@ -281,10 +287,12 @@
         )
         return jnp.dot(jnp.concatenate(tiles, axis=1), rhs, preferred_element_type=F32)
 
-    def multiply(p):
+    def multiply_theirs(p):
         for n in range(4):
             psend[p, :, 256 * n:256 * n + 256] = product(p, 1 - core, n).astype(BF)
         pair_copy(p).start()
+
+    def multiply_mine(p):
         for n in range(4):
             own[p, :, 256 * n:256 * n + 256] = product(p, core, n)
 
@@ -361,10 +369,14 @@
             ring(p, h, side).start()
         elif kind == "blocks":
             receive_blocks()
-        elif kind == "multiply":
+        elif kind == "compact":
+            compact_blocks()
+        elif kind == "theirs":
             for s in range(2):
                 ring_arrival(p, hops(p)[s], s)
-            multiply(p)
+            multiply_theirs(p)
+        elif kind == "mine":
+            multiply_mine(p)
         elif kind == "pair":
             pair_sum(p)
         elif kind == "first":
@@ -386,11 +398,11 @@
     dma = pltpu.SemaphoreType.DMA
     return pl.pallas_call(
         kernel,
-        out_shape=jax.ShapeDtypeStruct((128, 1024), BF),
+        out_shape=pltpu.VMEM((128, 1024), BF),
         in_specs=[smem, hbm, hbm, hbm, hbm],
         out_specs=pl.BlockSpec(memory_space=pltpu.VMEM),
         scratch_shapes=[
-            vmem((1, 1280), jnp.int32),
+            vmem((10, 128), jnp.int32),
             vmem((8, 1280), jnp.int32),
             vmem((8, 128), jnp.int32),
             pltpu.SMEM((8, 128), jnp.int32),
@@ -420,9 +432,9 @@
             dma((ROUNDS,)),
         ],
         compiler_params=pltpu.CompilerParams(
-            collective_id=0, has_side_effects=True, vmem_limit_bytes=66_000_000
+            collective_id=0, has_side_effects=True, vmem_limit_bytes=60_000_000
         ),
-    )(offsets, atom_of_slot.reshape(1, 1280), mask.T, coeffs, integrals)
+    )(offsets, atom_of_slot.reshape(10, 128), mask.T, coeffs, integrals)
 
 
 def solution(mesh):

time: 107 us -> 103 us (0.963)
  local copies, waits for them, and re-layouts: 2.96 us -> 0.71 us
  Pallas kernels: 104 us -> 102 us
    pallas_call x1, Pallas kernels: 104 us -> 102 us  [body(): pl.pallas_call(kernel, out_shape=pltpu.VMEM((128, 1024), BF), in_specs=[s...]
    reshape x1 -> x0, local copies, waits for them, and re-layouts: 1.29 us -> none  [body(): atom_of_slot.reshape(1, 1280)]
where the time goes in v4:
time: 103 us; the launch traced here: 102 us
  Pallas kernels  102 us (99%)
    pallas_call x1, Pallas kernels, body(): pl.pallas_call(kernel, out_shape=pltpu.VMEM((128, 1024), BF), in_specs=[s...  102 us

profile of v4, /device:TPU:1, one launch (start us, length us, event | category | flops | bytes accessed | tf_op | source)
XLA Modules:
  0.0 102.4 jit_solution(1113475406808045315)
XLA Ops:
  0.0 101.7 %shard_map.55 = bf16[128,1024]{1,0:T(8,128)(2,1)S(1)} custom-call(s32[1281]{0:T(1024)} %off_s.1, s32[10,128]{1,0:T(8,128)} %bitcast.3, s32[8,1280]{1,0:T(8,128)} %bitcast.2, bf16[1280,512]{1,0:T(8,128)(2,1)} %coef_hbm.1, bf16[40,32,1024]{2,1,0:T(8,128)(2,1)} %v_hbm.1), custom_call_target="tpu_custom_call" | custom-call | tf_op jit(solution)/shard_map/pallas_call | solution.py:399
  101.7 0.7 copy.7

commit v5 on v4

--- a/solution.py
+++ b/solution.py
@@ -109,7 +109,6 @@
     load_m = pltpu.make_async_copy(mask_hbm, mask, load_sem.at[3])
     load_h.start()
     load_m.start()
-    load_v.start()
 
     barrier = pltpu.get_barrier_semaphore()
 
@@ -139,15 +138,21 @@
     smat[896:960, :] = jnp.zeros((64, 512), BF)
     smat[1024:1088, :] = jnp.zeros((64, 512), BF)
 
+    one = lax.broadcasted_iota(jnp.int32, (256, 256), 0) == lax.broadcasted_iota(jnp.int32, (256, 256), 1)
+    eye = jnp.where(one, 1.0, 0.0).astype(BF)
+
     load_c.wait()
-    rho = lax.broadcasted_iota(jnp.int32, (512, 512), 0)
-    col = lax.broadcasted_iota(jnp.int32, (512, 512), 1)
-    want = (rho & 15) + 256 * ((rho >> 4) & 1) + 16 * ((rho >> 5) & 7) + 128 * (rho >> 8)
-    perm = jnp.where(col == want, 1.0, 0.0).astype(BF)
+    load_v.start()
     for b in range(5):
-        ct[:, 256 * b:256 * b + 256] = lax.dot_general(
-            perm, cin[256 * b:256 * b + 256, :], (((1,), (1,)), ((), ())), preferred_element_type=F32
-        ).astype(BF)
+        for half in range(2):
+            turned = lax.dot_general(
+                eye, cin[256 * b:256 * b + 256, 256 * half:256 * half + 256],
+                (((1,), (1,)), ((), ())), preferred_element_type=F32,
+            ).astype(BF)
+            for qc in range(2):
+                for p in range(ROUNDS):
+                    at = 256 * qc + 32 * p + 16 * half
+                    ct[at:at + 16, 256 * b:256 * b + 256] = turned[128 * qc + 16 * p:128 * qc + 16 * p + 16, :]
 
     def compact(r0, rw, k0, kw, c0, cw):
         return lax.dot_general(

time: 103 us -> 103 us (level)
  no operation moved by 1% of the time
where the time goes in v5:
time: 103 us; the launch traced here: 102 us
  Pallas kernels  102 us (99%)
    pallas_call x1, Pallas kernels, body(): pl.pallas_call(kernel, out_shape=pltpu.VMEM((128, 1024), BF), in_specs=[s...  102 us

profile of v5, /device:TPU:1, one launch (start us, length us, event | category | flops | bytes accessed | tf_op | source)
XLA Modules:
  0.0 102.4 jit_solution(17158924733685170016)
XLA Ops:
  0.0 101.7 %shard_map.55 = bf16[128,1024]{1,0:T(8,128)(2,1)S(1)} custom-call(s32[1281]{0:T(1024)} %off_s.1, s32[10,128]{1,0:T(8,128)} %bitcast.3, s32[8,1280]{1,0:T(8,128)} %bitcast.2, bf16[1280,512]{1,0:T(8,128)(2,1)} %coef_hbm.1, bf16[40,32,1024]{2,1,0:T(8,128)(2,1)} %v_hbm.1), custom_call_target="tpu_custom_call" | custom-call | tf_op jit(solution)/shard_map/pallas_call | solution.py:404
  101.7 0.7 copy.7

commit v6 on v5

--- a/solution.py
+++ b/solution.py
@@ -17,7 +17,7 @@
 START = 5.5
 SLOT = 2.65
 WIRE = 2.4
-V_READY = 55.5
+V_READY = 56.3
 LAG = 2
 
 

time: 103 us -> 103 us (level)
  no operation moved by 1% of the time
where the time goes in v6:
time: 103 us; the launch traced here: 102 us
  Pallas kernels  102 us (99%)
    pallas_call x1, Pallas kernels, body(): pl.pallas_call(kernel, out_shape=pltpu.VMEM((128, 1024), BF), in_specs=[s...  102 us

profile of v6, /device:TPU:1, one launch (start us, length us, event | category | flops | bytes accessed | tf_op | source)
XLA Modules:
  0.0 102.5 jit_solution(2557882930311149211)
XLA Ops:
  0.0 101.8 %shard_map.55 = bf16[128,1024]{1,0:T(8,128)(2,1)S(1)} custom-call(s32[1281]{0:T(1024)} %off_s.1, s32[10,128]{1,0:T(8,128)} %bitcast.3, s32[8,1280]{1,0:T(8,128)} %bitcast.2, bf16[1280,512]{1,0:T(8,128)(2,1)} %coef_hbm.1, bf16[40,32,1024]{2,1,0:T(8,128)(2,1)} %v_hbm.1), custom_call_target="tpu_custom_call" | custom-call | tf_op jit(solution)/shard_map/pallas_call | solution.py:404
  101.8 0.7 copy.7
